TPU v7x, 32 devices: a whole 2x2x4 slice. The times are simulated.
32 devices in a mesh: grp: 2 (over x), space: 16 (over z, y, core).
Axes of the slice: x: 2, y: 2, z: 4, core: 2. Of those that a mesh axis runs over, the one named last changes fastest.
Arguments:
- propagator: bfloat16 [4, 3, 4, 12, 32768], P('grp', None, None, None, 'space'), parts along dimension 0, may hold values from -6 to 6
- eigvecs: bfloat16 [4, 3, 256, 32768], P('grp', None, None, 'space'), parts along dimension 0, may hold values from -6 to 6
- operator_weights: float32 [256, 2, 256], P('grp'), parts along dimension 0, may hold values from -0.375 to 0.375
- sink_time: int32 [2], P('grp'), parts along dimension 0, may hold values from 0 to 127
- term_index: int32 [48, 3], replicated, may hold values from 0 to 11
- term_sign: int32 [48], replicated, may hold values from 0 to 1
- solver_order: int32 [32768], P('space'), may hold values from 0 to 32767, as said below
Outputs:
- solver_source: bfloat16 [4, 3, 4, 12, 32768], P('grp', None, None, None, 'space'), parts along dimension 0
There are 2 independent parts, one for each index of `grp`. A program takes and returns all parts, laid end to end along the dimension named above; an argument that names none is the same for every part. Nothing has to cross between parts.
Inputs may be any that keep to these rules, and one draw needn't show every extreme that they name: solver_order is a permutation of the sites; split into blocks of 2048 positions and each block into pieces of 128, piece d of block e holds only sites d * 2048 to (d + 1) * 2048 - 1.
All inputs are finite; a program needn't handle non-finite values.
Results may differ from a plain program's by a relative error of at most 0.006.
Values may be sent and summed in bfloat16 or wider, within the bound.
A program may use at most 64 MiB of HBM per device.

v0:
```python
import math
import jax
import jax.numpy as jnp
from jax import lax
from jax.sharding import PartitionSpec as P

NVEC = 256
NMOM = 4
EXTENT = 64
MOMENTA = ((0, 0, 0), (1, 0, 0), (0, 1, 0), (0, 0, 1))
PRECISE = lax.Precision.HIGHEST


def phase_tables(offset, length):
    site_index = offset + jnp.arange(length, dtype=jnp.int32)
    coord_x = site_index % EXTENT
    coord_y = site_index // EXTENT % EXTENT
    coord_z = site_index // (EXTENT * EXTENT)
    windings = jnp.stack(
        [
            (step_x * coord_x + step_y * coord_y + step_z * coord_z) % EXTENT
            for step_x, step_y, step_z in MOMENTA
        ]
    )
    angles = windings.astype(jnp.float32) * (2.0 * math.pi / EXTENT)
    return (jnp.cos(angles), jnp.sin(angles))


def phased_rows(prop_colour, cosine_table, sine_table):
    real_part = prop_colour[0].astype(jnp.float32)[None]
    imag_part = prop_colour[1].astype(jnp.float32)[None]
    cos_rows = cosine_table[:, None, None, :]
    sin_rows = sine_table[:, None, None, :]
    turned = jnp.stack(
        [cos_rows * real_part + sin_rows * imag_part, cos_rows * imag_part - sin_rows * real_part]
    )
    return turned.astype(jnp.bfloat16).reshape(-1, turned.shape[-1])


def project(eig_colour, phased, scale_in):
    site_dims = (((1,), (1,)), ((), ()))
    from_real = lax.dot_general(
        eig_colour[0], phased, site_dims, preferred_element_type=jnp.float32
    ).reshape(-1, 2, NMOM, 48)
    from_imag = lax.dot_general(
        eig_colour[1], phased, site_dims, preferred_element_type=jnp.float32
    ).reshape(-1, 2, NMOM, 48)
    real_part = from_real[:, 0] + from_imag[:, 1]
    imag_part = from_real[:, 1] - from_imag[:, 0]
    return jnp.stack([real_part, imag_part]) * scale_in


def assemble(pieces):
    stacked = jnp.stack(pieces)
    vectors = stacked.shape[2]
    return stacked.transpose(3, 1, 2, 0, 4).reshape(NMOM, 2, vectors, 144)


def weighted_total(blocks, weights):
    real_sum = jnp.einsum("k,pkc->pc", weights[0], blocks[:, 0], precision=PRECISE) - jnp.einsum(
        "k,pkc->pc", weights[1], blocks[:, 1], precision=PRECISE
    )
    imag_sum = jnp.einsum("k,pkc->pc", weights[0], blocks[:, 1], precision=PRECISE) + jnp.einsum(
        "k,pkc->pc", weights[1], blocks[:, 0], precision=PRECISE
    )
    return jnp.stack([real_sum, imag_sum], axis=1)


def term_tables(term_index, term_sign):
    channels = jnp.arange(12, dtype=jnp.int32)
    first_pick = (term_index[:, 0:1] == channels[None]).astype(jnp.float32)
    second_pick = (term_index[:, 1:2] == channels[None]).astype(jnp.float32)
    sign_values = (2 * term_sign - 1).astype(jnp.float32)
    placement = (term_index[None, :, 2] == channels[:, None]).astype(jnp.float32) * sign_values[
        None
    ]
    return (first_pick, second_pick, placement)


def contract(blocks, weighted, first_pick, second_pick, placement):
    vectors = blocks.shape[2]
    block_grid = blocks.reshape(NMOM, 2, vectors, 12, 12)
    first_terms = jnp.einsum("mi,pqkij->pqkmj", first_pick, block_grid, precision=PRECISE)
    second_terms = jnp.einsum(
        "mi,pqij->pqmj", second_pick, weighted.reshape(NMOM, 2, 12, 12), precision=PRECISE
    )[:, :, None]
    real_part = first_terms[:, 0] * second_terms[:, 0] - first_terms[:, 1] * second_terms[:, 1]
    imag_part = first_terms[:, 0] * second_terms[:, 1] + first_terms[:, 1] * second_terms[:, 0]
    product = jnp.stack([real_part, imag_part], axis=1)
    return jnp.einsum("cm,pqkmj->pqkcj", placement, product, precision=PRECISE).reshape(
        NMOM, 2, vectors, 144
    )


def rebuild(coeffs, eig_colour, colour, cosine_table, sine_table, scale_out):
    vectors = coeffs.shape[2]
    colour_block = coeffs.reshape(NMOM, 2, vectors, 3, 48)[:, :, :, colour]
    coeff_table = colour_block.transpose(2, 1, 0, 3).reshape(vectors, 2 * NMOM * 48)
    vector_dims = (((0,), (0,)), ((), ()))
    from_real = lax.dot_general(
        coeff_table, eig_colour[0], vector_dims, preferred_element_type=jnp.float32
    ).reshape(2, NMOM, 48, -1)
    from_imag = lax.dot_general(
        coeff_table, eig_colour[1], vector_dims, preferred_element_type=jnp.float32
    ).reshape(2, NMOM, 48, -1)
    real_part = from_real[0] - from_imag[1]
    imag_part = from_real[1] + from_imag[0]
    cos_rows = cosine_table[:, None, :]
    sin_rows = sine_table[:, None, :]
    out_real = jnp.sum(cos_rows * real_part - sin_rows * imag_part, axis=0)
    out_imag = jnp.sum(cos_rows * imag_part + sin_rows * real_part, axis=0)
    return jnp.stack([out_real, out_imag]) * scale_out


def on_device(
    propagator, eigvecs, operator_weights, sink_time, term_index, term_sign, solver_order
):
    length = propagator.shape[-1]
    devices = lax.axis_size("space")
    offset = lax.axis_index("space") * length
    cosine_table, sine_table = phase_tables(offset, length)
    scale_in = 1.0 / math.sqrt(3.0 * length * devices)
    pieces = []
    for colour in range(3):
        phased = phased_rows(propagator[:, colour], cosine_table, sine_table)
        pieces.append(project(eigvecs[:, colour], phased, scale_in))
    partial_blocks = assemble(pieces)
    weights = lax.dynamic_index_in_dim(operator_weights, sink_time[0], 0, keepdims=False)
    first_pick, second_pick, placement = term_tables(term_index, term_sign)
    blocks = lax.psum(partial_blocks, "space")
    weighted = weighted_total(blocks, weights)
    coeffs = contract(blocks, weighted, first_pick, second_pick, placement).astype(jnp.bfloat16)
    scale_out = 1.0 / math.sqrt(NMOM * NVEC)
    colours = [
        rebuild(coeffs, eigvecs[:, colour], colour, cosine_table, sine_table, scale_out)
        for colour in range(3)
    ]
    source = jnp.stack(colours, axis=1).astype(jnp.bfloat16).reshape(2 * 3 * 48, length)
    wanted = lax.all_to_all(
        solver_order.reshape(devices, -1), "space", split_axis=0, concat_axis=0, tiled=True
    )
    local_index = wanted.reshape(length) - offset
    picked = jnp.take(source, local_index, axis=1)
    placed = lax.all_to_all(picked, "space", split_axis=1, concat_axis=1, tiled=True)
    return placed.reshape(2, 3, 4, 12, length)


def solution(mesh):
    return jax.shard_map(
        on_device,
        mesh=mesh,
        in_specs=(
            P("grp", None, None, None, "space"),
            P("grp", None, None, "space"),
            P("grp", None, None),
            P("grp"),
            P(),
            P(),
            P("space"),
        ),
        out_specs=P("grp", None, None, None, "space"),
        check_vma=False,
    )
```

profile of v0, /device:TPU:0, one launch (start us, length us, event | category | flops | bytes accessed | tf_op | source)
XLA Modules:
  0.0 206.0 jit_solution(521534441980782932)
XLA Ops:
  6.8 1.5 bitcast_convert_fusion.5
  8.6 0.2 copy.38
  9.8 0.3 fusion.77
  10.0 2.7 %add_convert_fusion.2 = (bf16[1,4,4,12,2048]{4,3,2,1,0:T(8,128)(2,1)S(1)}, bf16[1,4,4,12,2048]{4,3,2,1,0:T(8,128)(2,1)S(1)}, bf16[1,4,4,12,2048]{4,3,2,1,0:T(8,1...) fusion(f32[4,12,2048]{2,1,0:T(8,128)S(1)} %copy.38, ...), kind=kLoop, calls=%fused_computation.16 | loop fusion | flops 9437184 | bytes 7143424 | tf_op jit(solution)/shard_map/convert.13
  12.8 0.3 pad_maximum_fusion
  13.1 1.4 convert_element_type.148
  14.4 3.2 %fusion.33 = f32[384,256]{1,0:T(8,128)} fusion(bf16[384,2048]{1,0:T(8,128)(2,1)} %convert_element_type.148, bf16[2,3,256,2048]{3,2,1,0:T(8,128)(2,1)} %param.8), kind=kOutput, calls=%fused_computation.58 | convolution fusion | flops 402653184 | bytes 3014656 | tf_op jit(solution)/shard_map/dot_general | solution.py:42
  17.6 2.7 %fusion.29 = f32[384,256]{1,0:T(8,128)} fusion(bf16[384,2048]{1,0:T(8,128)(2,1)S(1)} %copy-done.6, bf16[2,3,256,2048]{3,2,1,0:T(8,128)(2,1)} %param.8), kind=kOutput, calls=%fused_computation.54 | convolution fusion | flops 402653184 | bytes 3014656 | tf_op jit(solution)/shard_map/dot_general | solution.py:45
  20.4 0.3 pad_maximum_fusion.1
  20.6 1.4 convert_element_type.153
  22.0 3.2 %fusion.25 = f32[384,256]{1,0:T(8,128)} fusion(bf16[384,2048]{1,0:T(8,128)(2,1)} %convert_element_type.153, bf16[2,3,256,2048]{3,2,1,0:T(8,128)(2,1)} %param.8), kind=kOutput, calls=%fused_computation.50 | convolution fusion | flops 402653184 | bytes 3014656 | tf_op jit(solution)/shard_map/dot_general | solution.py:42
  25.2 2.7 %fusion.21 = f32[384,256]{1,0:T(8,128)} fusion(bf16[384,2048]{1,0:T(8,128)(2,1)S(1)} %copy-done.7, bf16[2,3,256,2048]{3,2,1,0:T(8,128)(2,1)} %param.8), kind=kOutput, calls=%fused_computation.46 | convolution fusion | flops 402653184 | bytes 3014656 | tf_op jit(solution)/shard_map/dot_general | solution.py:45
  27.9 0.3 pad_maximum_fusion.2
  28.2 1.4 convert_element_type.158
  29.5 2.4 %fusion.17 = f32[384,256]{1,0:T(8,128)S(1)} fusion(bf16[384,2048]{1,0:T(8,128)(2,1)} %convert_element_type.158, bf16[2,3,256,2048]{3,2,1,0:T(8,128)(2,1)} %param.8), kind=kOutput, calls=%fused_computation.42 | convolution fusion | flops 402653184 | bytes 3014656 | tf_op jit(solution)/shard_map/dot_general | solution.py:42
  32.0 1.9 fusion.13
  34.0 0.8 copy-done.9
  35.2 1.1 pad_maximum_fusion.3
  36.4 7.4 %all-to-all-start = ((s32[16,1,128]{2,1,0:T(1,128)}), s32[16,1,128]{2,1,0:T(1,128)S(1)}, u32[]{:S(2)}, u32[]{:S(2)}) async-start(s32[16,1,128]{2,1,0:T(1,128)} %bitcast), calls=%async_computation | async-start | bytes 16384 | tf_op jit(solution)/shard_map/all_to_all | solution.py:139
  44.5 5.7 %all-to-all-done = s32[16,1,128]{2,1,0:T(1,128)S(1)} async-done(((s32[16,1,128]{2,1,0:T(1,128)}), s32[16,1,128]{2,1,0:T(1,128)S(1)}, u32[]{:S(2)}, u32[]{:S(2)}) %all-to-all-start) | async-done | bytes 8224 | tf_op jit(solution)/shard_map/all_to_all | solution.py:139
  50.2 83.1 %all-reduce.2.cloned.1.call-done = f32[4,2,256,144]{2,3,1,0:T(8,128)} async-done(((f32[4,2,256,144]{2,3,1,0:T(8,128)}), f32[4,2,256,144]{2,3,1,0:T(8,128)}) %all-reduce.2.cloned.1.call-update) | async-done | bytes 1179664 | tf_op jit(solution)/shard_map/psum | solution.py:130
  133.4 1.7 fusion.51
  135.1 1.7 fusion.53
  137.0 0.6 fusion.50
  137.6 0.6 fusion.52
  138.6 0.9 copy.46
  139.5 2.1 %convolution_bitcast_fusion = f32[4,2,256,48,12]{2,3,4,1,0:T(8,128)S(1)} fusion(f32[4,2,256,12,12]{2,1,4,3,0:T(2,128)S(1)} %bitcast.204, s32[48]{0:T(128)S(1)} %get-tuple-element.55), kind=kOutput, calls=%fused_computation.7 | convolution fusion | flops 169869888 | bytes 5898432 | tf_op jit(solution)/shard_map/mi,pqkij->pqkmj/dot_general | solution.py:83
  141.7 0.9 multiply_subtract_fusion
  142.5 2.5 %fusion.8 = bf16[4,2,256,12,12]{2,3,4,1,0:T(8,128)(2,1)S(1)} fusion(f32[4,1,256,48,12]{2,3,4,1,0:T(8,128)S(1)} %get-tuple-element.24, f32[4,1,256,48,12]{2,3,4,1,0:T(8,128)S(1)} %get-tuple-element.23, f32[48]{0:T(128)S(1)} %add_convert_fusion.4, s32[48]{0:T(128)S(1)} %get-tuple-element.54), kind=kOutput, calls=%fused_computation.31 | convolution fusion | flops 171345024 | bytes 5308800 | tf_op jit(solution)/shard_map/cm,pqkmj->pqkcj/dot_general | solution.py:90
  145.1 0.6 copy.50
  145.7 0.5 fusion.86
  146.3 0.6 fusion.11
  146.8 0.6 fusion.15
  147.5 0.6 fusion.19
  148.0 0.6 fusion.23
  148.7 0.6 fusion.27
  149.2 0.6 fusion.31
  149.8 0.6 slice_add_fusion
  150.5 0.7 slice_add_fusion.1
  151.2 0.7 slice_subtract_fusion.2
  151.8 1.4 subtract_reduce_fusion.2
  153.6 0.8 copy.57
  154.4 7.5 %gather_fusion = bf16[2048,288]{1,0:T(8,128)(2,1)S(1)} fusion(bf16[288,2048]{0,1:T(8,128)(2,1)S(1)} %copy.57, s32[2048]{0:T(1024)S(1)} %broadcast_clamp_fusion), kind=kCustom, calls=%fused_computation | custom fusion | bytes 2367488 | tf_op jit(solution)/shard_map/jit(_take)/gather | solution.py:143
  161.9 0.9 copy.58
  162.9 33.0 %all_to_all.15 = bf16[288,16,128]{2,0,1:T(8,128)(2,1)S(1)} all-to-all(bf16[288,16,128]{2,0,1:T(8,128)(2,1)S(1)} %broadcast_select_fusion), channel_id=1, replica_groups=mesh['grp'=2,'space'=16] {'space'}, dimensions={1} | all-to-all | bytes 2359296 | tf_op jit(solution)/shard_map/all_to_all | solution.py:144
  195.9 0.5 copy.59
  196.4 0.8 reshape.956
  197.2 1.9 copy.60
  (71 shorter events, 2.9 us)
Async XLA Ops:
  6.5 126.8 %copy-start = (f32[128,2,256]{2,1,0:T(2,128)S(1)}, f32[128,2,256]{2,1,0:T(2,128)}, u32[]{:S(2)}) copy-start(f32[128,2,256]{2,1,0:T(2,128)} %param.9) | copy-start | bytes 786436
  6.5 126.8 %all-reduce.2.cloned.1.call-start = ((), (), s32[]{:S(2)}) async-start(), calls=%async_computation.2 | async-start | bytes 2359296 | tf_op jit(solution)/shard_map/psum | solution.py:130
  14.4 3.2 %copy-start.6 = (bf16[384,2048]{1,0:T(8,128)(2,1)S(1)}, bf16[384,2048]{1,0:T(8,128)(2,1)}, u32[]{:S(2)}) copy-start(bf16[384,2048]{1,0:T(8,128)(2,1)} %convert_element_type.148) | copy-start | bytes 4718596
  17.6 2.7 %copy-start.4 = (bf16[1,4,4,12,2048]{4,3,2,1,0:T(8,128)(2,1)S(1)}, bf16[1,4,4,12,2048]{4,3,2,1,0:T(8,128)(2,1)}, u32[]{:S(2)}) copy-start(bf16[1,4,4,12,2048]{4,3,2,1,0:T(8,128)(2,1)} %get-tuple-element.48) | copy-start | bytes 2359300
  17.6 2.7 %copy-start.5 = (bf16[1,4,4,12,2048]{4,3,2,1,0:T(8,128)(2,1)S(1)}, bf16[1,4,4,12,2048]{4,3,2,1,0:T(8,128)(2,1)}, u32[]{:S(2)}) copy-start(bf16[1,4,4,12,2048]{4,3,2,1,0:T(8,128)(2,1)} %get-tuple-element.49) | copy-start | bytes 2359300
  22.0 3.2 %copy-start.7 = (bf16[384,2048]{1,0:T(8,128)(2,1)S(1)}, bf16[384,2048]{1,0:T(8,128)(2,1)}, u32[]{:S(2)}) copy-start(bf16[384,2048]{1,0:T(8,128)(2,1)} %convert_element_type.153) | copy-start | bytes 4718596
  25.2 2.7 %copy-start.3 = (bf16[1,4,4,12,2048]{4,3,2,1,0:T(8,128)(2,1)S(1)}, bf16[1,4,4,12,2048]{4,3,2,1,0:T(8,128)(2,1)}, u32[]{:S(2)}) copy-start(bf16[1,4,4,12,2048]{4,3,2,1,0:T(8,128)(2,1)} %get-tuple-element.51) | copy-start | bytes 2359300
  29.5 2.4 %copy-start.8 = (bf16[384,2048]{1,0:T(8,128)(2,1)S(1)}, bf16[384,2048]{1,0:T(8,128)(2,1)}, u32[]{:S(2)}) copy-start(bf16[384,2048]{1,0:T(8,128)(2,1)} %convert_element_type.158) | copy-start | bytes 4718596
  32.0 2.0 copy-start.11
  32.0 2.0 copy-start.12
  33.9 1.0 copy-start.9
  33.9 1.1 copy-start.10
  35.2 8.6 %copy-start.13 = (s32[48,3]{0,1:T(4,128)S(1)}, s32[48,3]{0,1:T(4,128)}, u32[]{:S(2)}) copy-start(s32[48,3]{0,1:T(4,128)} %param.11) | copy-start | bytes 1732
  35.2 8.6 %copy-start.14 = (s32[48]{0:T(128)S(1)}, s32[48]{0:T(128)}, u32[]{:S(2)}) copy-start(s32[48]{0:T(128)} %param.12) | copy-start | bytes 580
  36.4 13.8 %all-to-all-start = ((s32[16,1,128]{2,1,0:T(1,128)}), s32[16,1,128]{2,1,0:T(1,128)S(1)}, u32[]{:S(2)}, u32[]{:S(2)}) async-start(s32[16,1,128]{2,1,0:T(1,128)} %bitcast), calls=%async_computation | async-start | bytes 16384 | tf_op jit(solution)/shard_map/all_to_all | solution.py:139
  133.4 3.6 %copy-start.2 = (f32[4,2,256,144]{2,3,1,0:T(8,128)S(1)}, f32[4,2,256,144]{2,3,1,0:T(8,128)}, u32[]{:S(2)}) copy-start(f32[4,2,256,144]{2,3,1,0:T(8,128)} %all-reduce.2.cloned.1.call-done) | copy-start | bytes 3538948
  139.5 6.7 %slice-start = ((s8[6291456]{0:T(1024)(128)(4,1)}), s8[4194304]{0:T(1024)(128)(4,1)S(1)}, s32[]{:S(2)}) async-start(s8[6291456]{0:T(1024)(128)(4,1)} %bitcast.211), calls=%async_computation.3 | async-start | bytes 8388608
  141.7 4.6 %slice-start.1 = ((s8[6291456]{0:T(1024)(128)(4,1)}), s8[2097152]{0:T(1024)(128)(4,1)S(1)}, s32[]{:S(2)}) async-start(s8[6291456]{0:T(1024)(128)(4,1)} %bitcast.211), calls=%async_computation.4 | async-start | bytes 4194304
  196.4 2.8 %copy-start.1 = (f32[128,2,256]{2,1,0:T(2,128)S(1)}, f32[128,2,256]{2,1,0:T(2,128)}, u32[]{:S(2)}) copy-start(f32[128,2,256]{2,1,0:T(2,128)} %param.9) | copy-start | bytes 786436
Sparse Core Ops, SparseCore 0:
  36.5 96.7 all-reduce.1
where the time goes:
time: 206 us
  waiting for transfers between devices  88.8 us (43%)
  blocking collectives  33 us (16%)
  matrix products  29 us (14%)
  local copies, waits for them, and re-layouts  21.5 us (10%)
  between operations  14.6 us (7%)
  other arithmetic  11.7 us (6%)
  starting transfers between devices  7.44 us (4%)
    psum x1, waiting for transfers between devices, on_device(): blocks = lax.psum(partial_blocks, 'space')  83.1 us
    all_to_all x1, blocking collectives, on_device(): lax.all_to_all(picked, 'space', split_axis=1, concat_axis=1, tiled=True)  33 us
    dot_general x3, matrix products, project(): lax.dot_general(eig_colour[0], phased, site_dims, preferred_element_type=...  8.78 us
    gather x2, local copies, waits for them, and re-layouts, on_device(): picked = jnp.take(source, local_index, axis=1)  8.36 us
    all_to_all x1, starting transfers between devices, on_device(): lax.all_to_all(solver_order.reshape(devices, -1), 'space', split_axis=0,...  7.43 us
    dot_general x3, matrix products, project(): lax.dot_general(eig_colour[1], phased, site_dims, preferred_element_type=...  7.31 us
    all_to_all x1, waiting for transfers between devices, on_device(): lax.all_to_all(solver_order.reshape(devices, -1), 'space', split_axis=0,...  5.65 us
    convert_element_type x3, local copies, waits for them, and re-layouts, phased_rows(): return turned.astype(jnp.bfloat16).reshape(-1, turned.shape[-1])  4.12 us
  transfers between devices with their start and end apart: 2, of which 2 were waited for; matrix products, arithmetic and copies ran while one was open for 0% of the time, Pallas kernels for 0%

commit v1 on v0

--- a/solution.py
+++ b/solution.py
@@ -127,7 +127,7 @@
     partial_blocks = assemble(pieces)
     weights = lax.dynamic_index_in_dim(operator_weights, sink_time[0], 0, keepdims=False)
     first_pick, second_pick, placement = term_tables(term_index, term_sign)
-    blocks = lax.psum(partial_blocks, "space")
+    blocks = jnp.sum(lax.all_gather(partial_blocks, "space"), axis=0)
     weighted = weighted_total(blocks, weights)
     coeffs = contract(blocks, weighted, first_pick, second_pick, placement).astype(jnp.bfloat16)
     scale_out = 1.0 / math.sqrt(NMOM * NVEC)

time: 206 us -> 218 us (1.058)
  other arithmetic: 11.7 us -> 19.7 us
  waiting for transfers between devices: 88.8 us -> 93.7 us
  matrix products: 29 us -> 26.8 us
    all_gather x0 -> x1, waiting for transfers between devices: none -> 87.8 us  [on_device(): blocks = jnp.sum(lax.all_gather(partial_blocks, 'space'), axis=0)]
    psum x1 -> x0, waiting for transfers between devices: 83.1 us -> none  [on_device(): blocks = lax.psum(partial_blocks, 'space')]
    reduce_sum x0 -> x1, other arithmetic: none -> 7.76 us  [on_device(): blocks = jnp.sum(lax.all_gather(partial_blocks, 'space'), axis=0)]
where the time goes in v1:
time: 218 us
  waiting for transfers between devices  93.7 us (43%)
  blocking collectives  33.9 us (16%)
  matrix products  26.8 us (12%)
  local copies, waits for them, and re-layouts  21.4 us (10%)
  other arithmetic  19.7 us (9%)
  between operations  14.6 us (7%)
  starting transfers between devices  7.44 us (3%)
    all_gather x1, waiting for transfers between devices, on_device(): blocks = jnp.sum(lax.all_gather(partial_blocks, 'space'), axis=0)  87.8 us
    all_to_all x1, blocking collectives, on_device(): lax.all_to_all(picked, 'space', split_axis=1, concat_axis=1, tiled=True)  33.9 us
    dot_general x3, matrix products, project(): lax.dot_general(eig_colour[0], phased, site_dims, preferred_element_type=...  8.77 us
    gather x2, local copies, waits for them, and re-layouts, on_device(): picked = jnp.take(source, local_index, axis=1)  8.36 us
    reduce_sum x1, other arithmetic, on_device(): blocks = jnp.sum(lax.all_gather(partial_blocks, 'space'), axis=0)  7.76 us
    all_to_all x1, starting transfers between devices, on_device(): lax.all_to_all(solver_order.reshape(devices, -1), 'space', split_axis=0,...  7.43 us
    dot_general x3, matrix products, project(): lax.dot_general(eig_colour[1], phased, site_dims, preferred_element_type=...  7.3 us
    all_to_all x1, waiting for transfers between devices, on_device(): lax.all_to_all(solver_order.reshape(devices, -1), 'space', split_axis=0,...  5.82 us
  transfers between devices with their start and end apart: 2, of which 2 were waited for; matrix products, arithmetic and copies ran while one was open for 0% of the time, Pallas kernels for 0%

profile of v1, /device:TPU:0, one launch (start us, length us, event | category | flops | bytes accessed | tf_op | source)
XLA Modules:
  0.0 217.6 jit_solution(5489960956661115282)
XLA Ops:
  6.8 1.5 bitcast_convert_fusion.5
  9.8 0.3 fusion.77
  10.0 2.8 %add_convert_fusion.2 = (bf16[1,4,4,12,2048]{4,3,2,1,0:T(8,128)(2,1)S(1)}, bf16[1,4,4,12,2048]{4,3,2,1,0:T(8,128)(2,1)S(1)}, bf16[1,4,4,12,2048]{4,3,2,1,0:T(8,1...) fusion(f32[4,12,2048]{2,1,0:T(8,128)S(1)} %copy.37, ...), kind=kLoop, calls=%fused_computation.16 | loop fusion | flops 9437184 | bytes 7143424 | tf_op jit(solution)/shard_map/convert.13
  12.8 0.3 pad_maximum_fusion
  13.1 1.4 convert_element_type.148
  14.5 3.2 %fusion.33 = f32[384,256]{1,0:T(8,128)} fusion(bf16[384,2048]{1,0:T(8,128)(2,1)} %convert_element_type.148, bf16[2,3,256,2048]{3,2,1,0:T(8,128)(2,1)} %param.8), kind=kOutput, calls=%fused_computation.58 | convolution fusion | flops 402653184 | bytes 3014656 | tf_op jit(solution)/shard_map/dot_general | solution.py:42
  17.6 2.7 %fusion.29 = f32[384,256]{1,0:T(8,128)} fusion(bf16[384,2048]{1,0:T(8,128)(2,1)S(1)} %copy-done.5, bf16[2,3,256,2048]{3,2,1,0:T(8,128)(2,1)} %param.8), kind=kOutput, calls=%fused_computation.54 | convolution fusion | flops 402653184 | bytes 3014656 | tf_op jit(solution)/shard_map/dot_general | solution.py:45
  20.4 0.3 pad_maximum_fusion.1
  20.6 1.4 convert_element_type.153
  22.0 3.2 %fusion.25 = f32[384,256]{1,0:T(8,128)} fusion(bf16[384,2048]{1,0:T(8,128)(2,1)} %convert_element_type.153, bf16[2,3,256,2048]{3,2,1,0:T(8,128)(2,1)} %param.8), kind=kOutput, calls=%fused_computation.50 | convolution fusion | flops 402653184 | bytes 3014656 | tf_op jit(solution)/shard_map/dot_general | solution.py:42
  25.2 2.7 %fusion.21 = f32[384,256]{1,0:T(8,128)} fusion(bf16[384,2048]{1,0:T(8,128)(2,1)S(1)} %copy-done.6, bf16[2,3,256,2048]{3,2,1,0:T(8,128)(2,1)} %param.8), kind=kOutput, calls=%fused_computation.46 | convolution fusion | flops 402653184 | bytes 3014656 | tf_op jit(solution)/shard_map/dot_general | solution.py:45
  27.9 0.3 pad_maximum_fusion.2
  28.1 1.4 convert_element_type.158
  29.5 2.4 %fusion.17 = f32[384,256]{1,0:T(8,128)S(1)} fusion(bf16[384,2048]{1,0:T(8,128)(2,1)} %convert_element_type.158, bf16[2,3,256,2048]{3,2,1,0:T(8,128)(2,1)} %param.8), kind=kOutput, calls=%fused_computation.42 | convolution fusion | flops 402653184 | bytes 3014656 | tf_op jit(solution)/shard_map/dot_general | solution.py:42
  32.0 1.9 fusion.13
  34.0 0.8 copy-done.8
  35.2 1.1 pad_maximum_fusion.3
  36.4 7.4 %all-to-all-start = ((s32[16,1,128]{2,1,0:T(1,128)}), s32[16,1,128]{2,1,0:T(1,128)S(1)}, u32[]{:S(2)}, u32[]{:S(2)}) async-start(s32[16,1,128]{2,1,0:T(1,128)} %bitcast), calls=%async_computation | async-start | bytes 16384 | tf_op jit(solution)/shard_map/all_to_all | solution.py:139
  44.5 5.8 %all-to-all-done = s32[16,1,128]{2,1,0:T(1,128)S(1)} async-done(((s32[16,1,128]{2,1,0:T(1,128)}), s32[16,1,128]{2,1,0:T(1,128)S(1)}, u32[]{:S(2)}, u32[]{:S(2)}) %all-to-all-start) | async-done | bytes 8224 | tf_op jit(solution)/shard_map/all_to_all | solution.py:139
  50.4 87.8 %all-gather.2.cloned.1.call-done = f32[16,4,2,256,144]{3,4,2,1,0:T(8,128)} async-done(((f32[1,4,2,256,144]{3,4,2,1,0:T(8,128)}), f32[16,4,2,256,144]{3,4,2,1,0:T(8,128)}) %all-gather.2.cloned.1.call-update) | async-done | bytes 18874384 | tf_op jit(solution)/shard_map/all_gather | solution.py:130
  138.2 7.8 %reduce_sum.63 = f32[4,2,256,144]{2,3,1,0:T(8,128)S(1)} reduce(f32[16,4,2,256,144]{3,4,2,1,0:T(8,128)} %all-gather.2.cloned.1.call-done, f32[]{:T(128)} %constant.102.clone.1), dimensions={0}, to_apply=%region_0.1 | reduce | flops 4423680 | bytes 20054020 | tf_op jit(solution)/shard_map/reduce_sum | solution.py:130
  146.0 0.6 fusion.51
  146.6 0.6 fusion.53
  147.2 0.6 fusion.50
  147.8 0.6 fusion.52
  148.4 0.9 copy.45
  149.9 2.1 convolution_bitcast_fusion
  152.1 1.1 multiply_subtract_fusion
  153.2 2.5 %fusion.8 = bf16[4,2,256,12,12]{2,3,4,1,0:T(8,128)(2,1)S(1)} fusion(f32[4,1,256,48,12]{2,3,4,1,0:T(8,128)S(1)} %get-tuple-element.24, f32[4,1,256,48,12]{2,3,4,1,0:T(8,128)S(1)} %get-tuple-element.23, f32[48]{0:T(128)S(1)} %add_convert_fusion.4, s32[48]{0:T(128)S(1)} %get-tuple-element.54), kind=kOutput, calls=%fused_computation.31 | convolution fusion | flops 171345024 | bytes 5308800 | tf_op jit(solution)/shard_map/cm,pqkmj->pqkcj/dot_general | solution.py:90
  155.7 0.6 copy.49
  156.3 0.5 fusion.86
  156.9 0.6 fusion.11
  157.5 0.6 fusion.15
  158.1 0.6 fusion.19
  158.7 0.6 fusion.23
  159.3 0.6 fusion.27
  159.9 0.6 fusion.31
  160.4 0.6 slice_add_fusion
  161.1 0.7 slice_add_fusion.1
  161.8 0.7 slice_subtract_fusion.2
  162.5 1.4 subtract_reduce_fusion.2
  164.2 0.8 copy.56
  165.0 7.5 %gather_fusion = bf16[2048,288]{1,0:T(8,128)(2,1)S(1)} fusion(bf16[288,2048]{0,1:T(8,128)(2,1)S(1)} %copy.56, s32[2048]{0:T(1024)S(1)} %broadcast_clamp_fusion), kind=kCustom, calls=%fused_computation | custom fusion | bytes 2367488 | tf_op jit(solution)/shard_map/jit(_take)/gather | solution.py:143
  172.5 0.9 copy.57
  173.5 33.9 %all_to_all.15 = bf16[288,16,128]{2,0,1:T(8,128)(2,1)S(1)} all-to-all(bf16[288,16,128]{2,0,1:T(8,128)(2,1)S(1)} %broadcast_select_fusion), channel_id=1, replica_groups=mesh['grp'=2,'space'=16] {'space'}, dimensions={1} | all-to-all | bytes 2359296 | tf_op jit(solution)/shard_map/all_to_all | solution.py:144
  207.5 0.5 copy.58
  208.0 0.8 reshape.952
  208.8 1.9 copy.59
  (70 shorter events, 3.2 us)
Async XLA Ops:
  6.5 139.5 %copy-start = (f32[128,2,256]{2,1,0:T(2,128)S(1)}, f32[128,2,256]{2,1,0:T(2,128)}, u32[]{:S(2)}) copy-start(f32[128,2,256]{2,1,0:T(2,128)} %param.9) | copy-start | bytes 786436
  6.5 131.7 %all-gather.2.cloned.1.call-start = ((), (), s32[]{:S(2)}) async-start(), calls=%async_computation.2 | async-start | bytes 20054016 | tf_op jit(solution)/shard_map/all_gather | solution.py:130
  14.5 3.2 %copy-start.5 = (bf16[384,2048]{1,0:T(8,128)(2,1)S(1)}, bf16[384,2048]{1,0:T(8,128)(2,1)}, u32[]{:S(2)}) copy-start(bf16[384,2048]{1,0:T(8,128)(2,1)} %convert_element_type.148) | copy-start | bytes 4718596
  17.6 2.7 %copy-start.3 = (bf16[1,4,4,12,2048]{4,3,2,1,0:T(8,128)(2,1)S(1)}, bf16[1,4,4,12,2048]{4,3,2,1,0:T(8,128)(2,1)}, u32[]{:S(2)}) copy-start(bf16[1,4,4,12,2048]{4,3,2,1,0:T(8,128)(2,1)} %get-tuple-element.48) | copy-start | bytes 2359300
  17.6 2.7 %copy-start.4 = (bf16[1,4,4,12,2048]{4,3,2,1,0:T(8,128)(2,1)S(1)}, bf16[1,4,4,12,2048]{4,3,2,1,0:T(8,128)(2,1)}, u32[]{:S(2)}) copy-start(bf16[1,4,4,12,2048]{4,3,2,1,0:T(8,128)(2,1)} %get-tuple-element.49) | copy-start | bytes 2359300
  22.0 3.2 %copy-start.6 = (bf16[384,2048]{1,0:T(8,128)(2,1)S(1)}, bf16[384,2048]{1,0:T(8,128)(2,1)}, u32[]{:S(2)}) copy-start(bf16[384,2048]{1,0:T(8,128)(2,1)} %convert_element_type.153) | copy-start | bytes 4718596
  25.2 2.7 %copy-start.2 = (bf16[1,4,4,12,2048]{4,3,2,1,0:T(8,128)(2,1)S(1)}, bf16[1,4,4,12,2048]{4,3,2,1,0:T(8,128)(2,1)}, u32[]{:S(2)}) copy-start(bf16[1,4,4,12,2048]{4,3,2,1,0:T(8,128)(2,1)} %get-tuple-element.51) | copy-start | bytes 2359300
  29.5 2.4 %copy-start.7 = (bf16[384,2048]{1,0:T(8,128)(2,1)S(1)}, bf16[384,2048]{1,0:T(8,128)(2,1)}, u32[]{:S(2)}) copy-start(bf16[384,2048]{1,0:T(8,128)(2,1)} %convert_element_type.158) | copy-start | bytes 4718596
  32.0 2.0 copy-start.10
  32.0 2.0 copy-start.11
  33.9 1.0 copy-start.8
  33.9 1.1 copy-start.9
  35.2 8.6 %copy-start.12 = (s32[48,3]{0,1:T(4,128)S(1)}, s32[48,3]{0,1:T(4,128)}, u32[]{:S(2)}) copy-start(s32[48,3]{0,1:T(4,128)} %param.11) | copy-start | bytes 1732
  35.2 8.6 %copy-start.13 = (s32[48]{0:T(128)S(1)}, s32[48]{0:T(128)}, u32[]{:S(2)}) copy-start(s32[48]{0:T(128)} %param.12) | copy-start | bytes 580
  36.4 14.0 %all-to-all-start = ((s32[16,1,128]{2,1,0:T(1,128)}), s32[16,1,128]{2,1,0:T(1,128)S(1)}, u32[]{:S(2)}, u32[]{:S(2)}) async-start(s32[16,1,128]{2,1,0:T(1,128)} %bitcast), calls=%async_computation | async-start | bytes 16384 | tf_op jit(solution)/shard_map/all_to_all | solution.py:139
  149.9 6.9 %slice-start = ((s8[6291456]{0:T(1024)(128)(4,1)}), s8[4194304]{0:T(1024)(128)(4,1)S(1)}, s32[]{:S(2)}) async-start(s8[6291456]{0:T(1024)(128)(4,1)} %bitcast.211), calls=%async_computation.3 | async-start | bytes 8388608
  152.0 4.8 %slice-start.1 = ((s8[6291456]{0:T(1024)(128)(4,1)}), s8[2097152]{0:T(1024)(128)(4,1)S(1)}, s32[]{:S(2)}) async-start(s8[6291456]{0:T(1024)(128)(4,1)} %bitcast.211), calls=%async_computation.4 | async-start | bytes 4194304
  208.0 2.8 %copy-start.1 = (f32[128,2,256]{2,1,0:T(2,128)S(1)}, f32[128,2,256]{2,1,0:T(2,128)}, u32[]{:S(2)}) copy-start(f32[128,2,256]{2,1,0:T(2,128)} %param.9) | copy-start | bytes 786436
Sparse Core Ops, SparseCore 0:
  36.5 101.6 all-gather.1
